TPU v7x, 16 devices: a 4x2x1 block of a 4x4x8 slice. The times are simulated.
16 devices in a mesh: rep: 4 (over y, z, core), dp: 4 (over x).
Axes of the slice: x: 4, y: 2, z: 1, core: 2. Of those that a mesh axis runs over, the one named last changes fastest.
The devices are a block of a 4x4x8 slice.
Arguments:
- x: bfloat16 [16, 4096, 512], P(('rep', 'dp')), parts along dimension 0
- dy: bfloat16 [16, 4096, 512], P(('rep', 'dp')), parts along dimension 0
- w_gate: bfloat16 [2, 512, 2048], replicated
- w_up: bfloat16 [2, 512, 2048], replicated
- w_down: bfloat16 [2, 2048, 512], replicated
- m_w_gate: float32 [2, 512, 2048], replicated
- m_w_up: float32 [2, 512, 2048], replicated
- m_w_down: float32 [2, 2048, 512], replicated
- v_w_gate: float32 [2, 512, 2048], replicated
- v_w_up: float32 [2, 512, 2048], replicated
- v_w_down: float32 [2, 2048, 512], replicated
Outputs:
- output 1: bfloat16 [8, 512, 2048], P('rep'), parts along dimension 0
- output 2: bfloat16 [8, 512, 2048], P('rep'), parts along dimension 0
- output 3: bfloat16 [8, 2048, 512], P('rep'), parts along dimension 0
- output 4: float32 [8, 512, 2048], P('rep'), parts along dimension 0
- output 5: float32 [8, 512, 2048], P('rep'), parts along dimension 0
- output 6: float32 [8, 2048, 512], P('rep'), parts along dimension 0
- output 7: float32 [8, 512, 2048], P('rep'), parts along dimension 0
- output 8: float32 [8, 512, 2048], P('rep'), parts along dimension 0
- output 9: float32 [8, 2048, 512], P('rep'), parts along dimension 0
There are 4 independent parts. A program takes and returns all parts, laid end to end along the dimension named above; an argument that names none is the same for every part.
All inputs are finite; a program needn't handle non-finite values.
Results may differ from a plain program's by a relative error of at most 0.02.
Values are sent between devices in bfloat16 or wider.
A program may use at most 768 MiB of HBM per device.

v0:
```python
import jax
import jax.numpy as jnp
from jax import lax
from jax.sharding import PartitionSpec as P

NAMES = ("w_gate", "w_up", "w_down")


def matmul(a, w):
    return jnp.dot(a, w, preferred_element_type=jnp.float32).astype(jnp.bfloat16)


def normed(h):
    wide = h.astype(jnp.float32)
    scale = lax.rsqrt(jnp.mean(wide**2, -1, keepdims=True) + 1e-6)
    return (wide * scale).astype(jnp.bfloat16)


def layer(h, w):
    a = normed(h)
    gate = jnp.dot(a, w["w_gate"], preferred_element_type=jnp.float32)
    up = jnp.dot(a, w["w_up"], preferred_element_type=jnp.float32)
    return h + matmul((jax.nn.silu(gate) * up).astype(jnp.bfloat16), w["w_down"])


def adamw(w, m, v, g):
    m = 0.9 * m + 0.1 * g
    v = 0.95 * v + 0.05 * g * g
    step = m * lax.rsqrt(v + 1e-8) + 0.1 * w
    return (w - 0.02 * step).astype(jnp.bfloat16), m, v


def solution(mesh):
    def step(x, dy, *arrays):
        weights, m, v = (arrays[i : i + 3] for i in (0, 3, 6))
        layers = weights[0].shape[0]
        h, kept = x[0], []
        for number in range(layers):
            kept.append(h)
            h = layer(h, {name: w[number] for name, w in zip(NAMES, weights, strict=True)})
        by_h, summed = dy[0], [None] * layers
        for number in reversed(range(layers)):
            _, back = jax.vjp(lambda w, h: layer(h, w), {name: w[number] for name, w in zip(NAMES, weights, strict=True)}, kept[number])
            by_w, by_h = back(by_h)
            summed[number] = [lax.psum(by_w[name], "dp") for name in NAMES]
        gradients = [jnp.stack([summed[number][i] for number in range(layers)]).astype(jnp.float32) for i in range(3)]
        new = [adamw(w.astype(jnp.float32), m, v, g) for w, m, v, g in zip(weights, m, v, gradients, strict=True)]
        return tuple(one[which] for which in range(3) for one in new)

    return jax.shard_map(
        step,
        mesh=mesh,
        in_specs=(P(("rep", "dp"), None, None),) * 2 + (P(None, None, None),) * 9,
        out_specs=(P("rep", None, None),) * 9,
        check_vma=False,
    )
```

profile of v0, /device:TPU:112, one launch (start us, length us, event | category | flops | bytes accessed | tf_op | source)
XLA Modules:
  0.0 626.0 jit_solution(15857815428202061698)
XLA Ops:
  7.2 0.1 all-reduce.3.cloned.1.call-start
  7.3 6.3 %copy.20 = bf16[1,4096,512]{1,2,0:T(8,128)(2,1)} copy(bf16[1,4096,512]{2,1,0:T(8,128)(2,1)} %param.11) | data formatting | bytes 8388608 | tf_op args[0]
  13.6 3.1 fusion.18
  16.7 0.0 copy-start.13
  16.7 6.3 %copy.21 = bf16[1,4096,512]{1,2,0:T(8,128)(2,1)} copy(bf16[1,4096,512]{2,1,0:T(8,128)(2,1)} %param.12) | data formatting | bytes 8388608 | tf_op args[1]
  23.0 0.0 copy-start.2
  23.0 15.1 %convolution_convert_fusion.1 = bf16[4096,2048]{1,0:T(8,128)(2,1)} fusion(bf16[1,4096,512]{2,1,0:T(8,128)(2,1)} %param.12, bf16[2,2048,512]{2,1,0:T(8,128)(2,1)} %param.15), kind=kOutput, calls=%fused_computation.25 | convolution fusion | flops 8598323200 | bytes 23068672 | tf_op jit(solution)/shard_map/transpose(jvp())/dot_general | solution.py:10
  38.1 0.0 copy-done.2
  38.1 0.0 copy-start.5
  38.1 17.8 %fusion.88 = f32[4096,2048]{1,0:T(8,128)} fusion(bf16[2,512,2048]{2,1,0:T(8,128)(2,1)S(1)} %copy-done.2, bf16[1,4096,512]{2,1,0:T(8,128)(2,1)} %param.11, f32[4096]{0:T(1024)S(1)} %add_rsqrt_fusion), kind=kOutput, calls=%fused_computation.103 | convolution fusion | flops 8596226048 | bytes 39862272 | tf_op jit(solution)/shard_map/dot_general | solution.py:21
  55.9 0.0 copy-done.13
  55.9 0.0 copy-done.5
  55.9 32.5 %multiply_convert_fusion.1 = (bf16[4096,2048]{1,0:T(8,128)(2,1)}, f32[4096,2048]{1,0:T(8,128)}) fusion(f32[4096,2048]{1,0:T(8,128)} %fusion.88, bf16[2,512,2048]{2,1,0:T(8,128)(2,1)S(1)} %copy-done.5, bf16[1,4096,512]{2,1,0:T(8,128)(2,1)} %param.11, f32[4096]{0:T(1024)S(1)} %add_rsqrt_fusion), kind=kOutput, calls=%fused_computation.17 | convolution fusion | flops 8646557696 | bytes 90193920 | tf_op jit(solution)/shard_map/dot_general | solution.py:22
  88.4 15.8 %fusion.34 = (f32[4096]{0:T(1024)S(1)}, bf16[4096,512]{0,1:T(8,128)(2,1)}) fusion(bf16[4096,2048]{1,0:T(8,128)(2,1)} %get-tuple-element.24, bf16[2,2048,512]{2,1,0:T(8,128)(2,1)} %param.15, bf16[1,4096,512]{1,2,0:T(8,128)(2,1)} %copy.20), kind=kOutput, calls=%fused_computation.64 | convolution fusion | flops 8600416256 | bytes 27279360 | tf_op jit(solution)/shard_map/dot_general | solution.py:10
  104.2 0.0 copy-start.11
  104.2 18.2 %fusion.75 = f32[4096,2048]{1,0:T(8,128)} fusion(bf16[4096,512]{0,1:T(8,128)(2,1)} %get-tuple-element.27, f32[4096]{0:T(1024)S(1)} %fusion.101, bf16[2,512,2048]{2,1,0:T(8,128)(2,1)} %param.14), kind=kOutput, calls=%fused_computation.92 | convolution fusion | flops 8596226048 | bytes 39862272 | tf_op jit(solution)/shard_map/jvp()/dot_general | solution.py:22
  122.4 0.0 copy-done.11
  122.4 41.0 %fusion.2 = (bf16[4096,2048]{1,0:T(8,128)(2,1)}, f32[4096,2048]{1,0:T(8,128)}) fusion(f32[4096,2048]{1,0:T(8,128)} %fusion.75, bf16[4096,2048]{1,0:T(8,128)(2,1)} %convolution_convert_fusion.1, bf16[2,512,2048]{2,1,0:T(8,128)(2,1)} %param.13, bf16[4096,512]{0,1:T(8,128)(2,1)} %get-tuple-element.27, f32[4096]{0:T(1024)S(1)} %fusion.101), kind=kOutput, calls=%fused_computation.8 | convolution fusion | flops 8696889344 | bytes 106971136 | tf_op jit(solution)/shard_map/jvp()/dot_general | solution.py:21
  163.4 0.0 copy-start.7
  163.4 26.0 %fusion.59 = bf16[1,2048,512]{2,1,0:T(8,128)(2,1)} fusion(bf16[1,4096,512]{2,1,0:T(8,128)(2,1)} %param.12, f32[4096,2048]{1,0:T(8,128)} %fusion.75, f32[4096,2048]{1,0:T(8,128)} %get-tuple-element.29), kind=kOutput, calls=%fused_computation.86 | convolution fusion | flops 8641314816 | bytes 73400320 | tf_op jit(solution)/shard_map/transpose(jvp())/dot_general | solution.py:10
  189.3 0.0 copy-done.7
  189.3 20.6 %fusion.62 = bf16[1,512,2048]{2,1,0:T(8,128)(2,1)} fusion(bf16[4096,2048]{1,0:T(8,128)(2,1)} %convolution_convert_fusion.1, bf16[4096,512]{0,1:T(8,128)(2,1)S(1)} %copy-done.7, f32[4096]{0:T(1024)S(1)} %fusion.101, f32[4096,2048]{1,0:T(8,128)} %get-tuple-element.29), kind=kOutput, calls=%fused_computation.87 | convolution fusion | flops 8647606272 | bytes 56639488 | tf_op jit(solution)/shard_map/transpose(jvp())/dot_general | solution.py:22
  209.9 21.8 %fusion.37 = bf16[4096,512]{0,1:T(8,128)(2,1)} fusion(bf16[4096,2048]{1,0:T(8,128)(2,1)} %convolution_convert_fusion.1, bf16[2,512,2048]{2,1,0:T(8,128)(2,1)} %param.14, f32[4096,2048]{1,0:T(8,128)} %get-tuple-element.29), kind=kOutput, calls=%fused_computation.68 | convolution fusion | flops 8642363392 | bytes 56623104 | tf_op jit(solution)/shard_map/transpose(jvp())/dot_general | solution.py:22
  231.7 0.0 copy-start.3
  231.7 0.0 copy-start.8
  231.7 14.9 %fusion.63 = bf16[1,512,2048]{2,1,0:T(8,128)(2,1)} fusion(bf16[4096,2048]{1,0:T(8,128)(2,1)} %get-tuple-element.28, bf16[4096,512]{0,1:T(8,128)(2,1)} %get-tuple-element.27, f32[4096]{0:T(1024)S(1)} %fusion.101), kind=kOutput, calls=%fused_computation.88 | convolution fusion | flops 8596226048 | bytes 23085056 | tf_op jit(solution)/shard_map/transpose(jvp())/dot_general | solution.py:21
  246.6 0.0 copy-done.3
  246.6 0.0 copy-done.8
  246.6 0.0 copy-start.12
  246.6 0.0 copy-start.1
  246.6 15.1 %fusion.36 = (f32[4096]{0:T(1024)S(1)}, bf16[4096,512]{0,1:T(8,128)(2,1)}) fusion(bf16[4096,512]{0,1:T(8,128)(2,1)S(1)} %copy-done.8, bf16[4096,512]{0,1:T(8,128)(2,1)} %fusion.37, bf16[4096,2048]{1,0:T(8,128)(2,1)} %get-tuple-element.28, bf16[2,512,2048]{2,1,0:T(8,128)(2,1)S(1)} %copy-done.3), kind=kOutput, calls=%fused_computation.66 | convolution fusion | flops 8600416256 | bytes 31473664 | tf_op jit(solution)/shard_map/transpose(jvp())/dot_general | solution.py:21
  261.7 0.0 copy-done.12
  261.7 0.0 copy-done.1
  261.7 4.3 fusion.42
  266.0 0.0 copy-start.9
  266.0 2.0 copy-done.9
  268.1 0.0 copy-start.10
  268.1 13.8 %fusion.64 = bf16[1,2048,512]{2,1,0:T(8,128)(2,1)} fusion(bf16[4096,2048]{1,0:T(8,128)(2,1)} %get-tuple-element.24, bf16[4096,512]{0,1:T(8,128)(2,1)S(1)} %fusion.42), kind=kOutput, calls=%fused_computation.89 | convolution fusion | flops 8590983168 | bytes 23068672 | tf_op jit(solution)/shard_map/transpose(jvp())/dot_general | solution.py:10
  281.8 0.0 copy-done.10
  281.8 0.0 copy-start
  281.8 0.0 copy-start.14
  281.9 14.8 %convolution_convert_fusion = bf16[4096,2048]{1,0:T(8,128)(2,1)} fusion(bf16[4096,512]{0,1:T(8,128)(2,1)} %copy-done.9, bf16[2,2048,512]{2,1,0:T(8,128)(2,1)S(1)} %copy-done.10), kind=kOutput, calls=%fused_computation.24 | convolution fusion | flops 8598323200 | bytes 23068672 | tf_op jit(solution)/shard_map/transpose(jvp())/dot_general | solution.py:10
  296.7 0.0 copy-done
  296.7 0.0 copy-done.14
  296.7 20.8 %fusion.65 = bf16[1,512,2048]{2,1,0:T(8,128)(2,1)} fusion(bf16[4096,2048]{1,0:T(8,128)(2,1)} %convolution_convert_fusion, f32[4096,2048]{1,0:T(8,128)} %fusion.88, bf16[1,4096,512]{1,2,0:T(8,128)(2,1)S(1)} %copy-done, f32[4096]{0:T(1024)S(1)} %copy-done.14), kind=kOutput, calls=%fused_computation.90 | convolution fusion | flops 8647606272 | bytes 56639488 | tf_op jit(solution)/shard_map/transpose(jvp())/dot_general | solution.py:22
  317.5 34.0 %fusion.68 = bf16[1,512,2048]{2,1,0:T(8,128)(2,1)} fusion(f32[4096,2048]{1,0:T(8,128)} %fusion.88, f32[4096,2048]{1,0:T(8,128)} %get-tuple-element.25, bf16[4096,2048]{1,0:T(8,128)(2,1)} %convolution_convert_fusion, bf16[1,4096,512]{1,2,0:T(8,128)(2,1)} %copy.20, f32[4096]{0:T(1024)S(1)} %copy-done.14), kind=kOutput, calls=%fused_computation.91 | convolution fusion | flops 8689549312 | bytes 90193920 | tf_op jit(solution)/shard_map/transpose(jvp())/dot_general | solution.py:21
  351.5 0.1 all-reduce.3.cloned.1.call-update
  351.6 222.7 %all-reduce.3.cloned.1.call-done = (bf16[1,512,2048]{2,1,0:T(8,128)(2,1)}, bf16[1,512,2048]{2,1,0:T(8,128)(2,1)}, bf16[1,512,2048]{2,1,0:T(8,128)(2,1)}, bf16[1,...) async-done(((bf16[1,512,2048]{2,1,0:T(8,128)(2,1)}, bf16[1,512,2048]{2,1,0:T(8,128)(2,1)}, bf16[1,512,2048]{2,1,0:T(8,128)(2,1)}, ...) | async-done | bytes 12582928 | tf_op jit(solution)/shard_map/psum | solution.py:45
  574.2 0.0 copy-start.4
  574.2 0.0 copy-start.6
  574.2 16.7 %fusion.29 = (bf16[2,2048,512]{2,1,0:T(8,128)(2,1)}, f32[2,2048,512]{2,1,0:T(8,128)}, f32[2,2048,512]{2,1,0:T(8,128)}) fusion(bf16[2,2048,512]{2,1,0:T(8,128)(2,1)} %param.15, bf16[1,2048,512]{2,1,0:T(8,128)(2,1)} %get-tuple-element.13, bf16[1,2048,512]{2,1,0:T(8,128)(2,1)} %get-tuple-element.14, f32[2,2048,512]{2,1,0:T(8,128)} %param.21, ...), kind=kLoop, calls=%fused_computation.59 | loop fusion | flops 39845888 | bytes 46137344 | tf_op jit(solution)/shard_map/convert_element_type | solution.py:30
  590.9 0.0 copy-done.4
  590.9 0.0 copy-done.6
  590.9 27.7 %fusion.17 = (bf16[2,512,2048]{2,1,0:T(8,128)(2,1)}, f32[2,512,2048]{2,1,0:T(8,128)}, f32[2,512,2048]{2,1,0:T(8,128)}, bf16[2,512,2048]{2,1,0:T(8,128)(2,1)}, f3...) fusion(bf16[2,512,2048]{2,1,0:T(8,128)(2,1)S(1)} %copy-done.4, bf16[1,512,2048]{2,1,0:T(8,128)(2,1)} %get-tuple-element.9, ...), kind=kLoop, calls=%fused_computation.47 | loop fusion | flops 79691776 | bytes 92274688 | tf_op jit(solution)/shard_map/convert_element_type | solution.py:30
  (3 shorter events, 0.0 us)
Async XLA Ops:
  7.2 567.0 %all-reduce.3.cloned.1.call-start = ((), (), s32[]{:S(2)}) async-start(), calls=%async_computation | async-start | bytes 25165824 | tf_op jit(solution)/shard_map/psum | solution.py:45
  16.7 39.2 %copy-start.13 = (f32[4096]{0:T(1024)}, f32[4096]{0:T(1024)S(1)}, u32[]{:S(2)}) copy-start(f32[4096]{0:T(1024)S(1)} %add_rsqrt_fusion) | copy-start | bytes 49156
  23.0 15.1 %copy-start.2 = (bf16[2,512,2048]{2,1,0:T(8,128)(2,1)S(1)}, bf16[2,512,2048]{2,1,0:T(8,128)(2,1)}, u32[]{:S(2)}) copy-start(bf16[2,512,2048]{2,1,0:T(8,128)(2,1)} %param.13) | copy-start | bytes 12582916
  38.1 17.8 %copy-start.5 = (bf16[2,512,2048]{2,1,0:T(8,128)(2,1)S(1)}, bf16[2,512,2048]{2,1,0:T(8,128)(2,1)}, u32[]{:S(2)}) copy-start(bf16[2,512,2048]{2,1,0:T(8,128)(2,1)} %param.14) | copy-start | bytes 12582916
  104.2 18.2 %copy-start.11 = (f32[4096]{0:T(1024)}, f32[4096]{0:T(1024)S(1)}, u32[]{:S(2)}) copy-start(f32[4096]{0:T(1024)S(1)} %get-tuple-element.26) | copy-start | bytes 49156
  163.4 26.0 %copy-start.7 = (bf16[4096,512]{0,1:T(8,128)(2,1)S(1)}, bf16[4096,512]{0,1:T(8,128)(2,1)}, u32[]{:S(2)}) copy-start(bf16[4096,512]{0,1:T(8,128)(2,1)} %get-tuple-element.27) | copy-start | bytes 12582916
  231.7 14.9 %copy-start.3 = (bf16[2,512,2048]{2,1,0:T(8,128)(2,1)S(1)}, bf16[2,512,2048]{2,1,0:T(8,128)(2,1)}, u32[]{:S(2)}) copy-start(bf16[2,512,2048]{2,1,0:T(8,128)(2,1)} %param.13) | copy-start | bytes 12582916
  231.7 14.9 %copy-start.8 = (bf16[4096,512]{0,1:T(8,128)(2,1)S(1)}, bf16[4096,512]{0,1:T(8,128)(2,1)}, u32[]{:S(2)}) copy-start(bf16[4096,512]{0,1:T(8,128)(2,1)} %get-tuple-element.27) | copy-start | bytes 12582916
  246.6 15.1 %copy-start.12 = (f32[4096]{0:T(1024)S(1)}, f32[4096]{0:T(1024)}, u32[]{:S(2)}) copy-start(f32[4096]{0:T(1024)} %copy-done.11) | copy-start | bytes 49156
  246.6 15.1 %copy-start.1 = (bf16[1,4096,512]{1,2,0:T(8,128)(2,1)S(1)}, bf16[1,4096,512]{1,2,0:T(8,128)(2,1)}, u32[]{:S(2)}) copy-start(bf16[1,4096,512]{1,2,0:T(8,128)(2,1)} %copy.21) | copy-start | bytes 12582916
  266.0 2.0 copy-start.9
  268.1 13.8 %copy-start.10 = (bf16[2,2048,512]{2,1,0:T(8,128)(2,1)S(1)}, bf16[2,2048,512]{2,1,0:T(8,128)(2,1)}, u32[]{:S(2)}) copy-start(bf16[2,2048,512]{2,1,0:T(8,128)(2,1)} %param.15) | copy-start | bytes 12582916
  281.8 14.8 %copy-start = (bf16[1,4096,512]{1,2,0:T(8,128)(2,1)S(1)}, bf16[1,4096,512]{1,2,0:T(8,128)(2,1)}, u32[]{:S(2)}) copy-start(bf16[1,4096,512]{1,2,0:T(8,128)(2,1)} %copy.20) | copy-start | bytes 12582916
  281.8 14.8 %copy-start.14 = (f32[4096]{0:T(1024)S(1)}, f32[4096]{0:T(1024)}, u32[]{:S(2)}) copy-start(f32[4096]{0:T(1024)} %copy-done.13) | copy-start | bytes 49156
  574.2 16.7 %copy-start.4 = (bf16[2,512,2048]{2,1,0:T(8,128)(2,1)S(1)}, bf16[2,512,2048]{2,1,0:T(8,128)(2,1)}, u32[]{:S(2)}) copy-start(bf16[2,512,2048]{2,1,0:T(8,128)(2,1)} %param.13) | copy-start | bytes 12582916
  574.2 16.7 %copy-start.6 = (bf16[2,512,2048]{2,1,0:T(8,128)(2,1)S(1)}, bf16[2,512,2048]{2,1,0:T(8,128)(2,1)}, u32[]{:S(2)}) copy-start(bf16[2,512,2048]{2,1,0:T(8,128)(2,1)} %param.14) | copy-start | bytes 12582916
Sparse Core Ops, SparseCore 0:
  351.7 222.5 all-reduce.2
where the time goes:
time: 634 us; the launch traced here: 626 us
  matrix products  322 us (51%)
  waiting for transfers between devices  223 us (35%)
  other arithmetic  51.8 us (8%)
  local copies, waits for them, and re-layouts  14.7 us (2%)
  between operations  14.7 us (2%)
    psum x1, waiting for transfers between devices, step(): summed[number] = [lax.psum(by_w[name], 'dp') for name in NAMES]  223 us
    dot_general x5, matrix products, layer(): gate = jnp.dot(a, w['w_gate'], preferred_element_type=jnp.float32)  123 us
    dot_general x5, matrix products, layer(): up = jnp.dot(a, w['w_up'], preferred_element_type=jnp.float32)  114 us
    dot_general x5, matrix products, matmul(): jnp.dot(a, w, preferred_element_type=jnp.float32).astype(jnp.bfloat16)  85.5 us
    convert_element_type x2, other arithmetic, adamw(): return ((w - 0.02 * step).astype(jnp.bfloat16), m, v)  44.4 us
    unnamed x32, local copies, waits for them, and re-layouts  14.7 us
  transfers between devices with their start and end apart: 1, of which 1 were waited for; matrix products, arithmetic and copies ran while one was open for 0% of the time, Pallas kernels for 0%

commit v1 on v0

v1 whole, which is shorter than its diff:
```python
import functools

import jax
import jax.numpy as jnp
from jax import lax
from jax.experimental import pallas as pl
from jax.experimental.pallas import tpu as pltpu
from jax.sharding import PartitionSpec as P

F32 = jnp.float32
BF16 = jnp.bfloat16
CHUNK = 256
TILE = 512
GSLOTS = 4


def dot(a, b):
    return jnp.dot(a, b, preferred_element_type=F32)


def dot_t(a, b):
    return lax.dot_general(a, b, (((1,), (1,)), ((), ())), preferred_element_type=F32)


def sigmoid(z):
    return 0.5 * jnp.tanh(0.5 * z) + 0.5


def norm_scale(wide):
    return lax.rsqrt(jnp.mean(wide * wide, -1, keepdims=True) + 1e-6)


def step_kernel(
    n, comm,
    x_hbm, dy_hbm, wg_hbm, wu_hbm, wd_hbm, g_hbm,
    a_all, a_t, d_all, d_t, da, h_all, hid_all, dgu_all, w0_gu, w0_d, s_gu, s_d, part, r1, r2, grad,
    in_sem, w_sem, out_sem, send_sem, recv_sem,
):
    tokens, width = h_all.shape
    layers, _, ff = wg_hbm.shape
    chunks = ff // CHUNK
    tiles = tokens // TILE
    total = layers * chunks
    rows = width // n
    half = rows // 2
    top = layers - 1
    me = lax.axis_index("dp")
    right, left = lax.rem(me + 1, n), lax.rem(me + n - 1, n)
    across = lax.rem(me + 2, n)

    def load(src, dst, sem):
        return pltpu.make_async_copy(src, dst, sem)

    first = [
        load(wg_hbm.at[0], w0_gu.at[0], in_sem.at[0]),
        load(wu_hbm.at[0], w0_gu.at[1], in_sem.at[1]),
        load(wd_hbm.at[0], w0_d, in_sem.at[2]),
    ]

    def x_load(t):
        r = pl.ds(pl.multiple_of(t * TILE, TILE), TILE)
        return load(x_hbm.at[0, r], a_all.at[0, r], in_sem.at[4 + 2 * t])

    def dy_load(t):
        r = pl.ds(pl.multiple_of(t * TILE, TILE), TILE)
        return load(dy_hbm.at[0, r], d_all.at[r], in_sem.at[5 + 2 * t])

    def w_loads(s):
        layer = top - s // chunks
        c = pl.ds(pl.multiple_of(lax.rem(s, chunks) * CHUNK, CHUNK), CHUNK)
        slot = lax.rem(s, 2)
        return [
            load(wg_hbm.at[layer, :, c], s_gu.at[slot, :, pl.ds(0, CHUNK)], w_sem.at[slot, 0]),
            load(wu_hbm.at[layer, :, c], s_gu.at[slot, :, pl.ds(CHUNK, CHUNK)], w_sem.at[slot, 1]),
            load(wd_hbm.at[layer, c], s_d.at[slot], w_sem.at[slot, 2]),
        ]

    x_load(0).start()
    for copy in first:
        copy.start()
    for t in range(1, tiles):
        x_load(t).start()
    for t in range(tiles):
        dy_load(t).start()
    for copy in w_loads(0):
        copy.start()
    if comm:
        barrier = pltpu.get_barrier_semaphore()
        for other in (left, right):
            pl.semaphore_signal(barrier, inc=1, device_id={"dp": other}, device_id_type=pl.DeviceIdType.MESH)
    x_load(0).wait()
    for copy in first:
        copy.wait()

    def forward(t, carry):
        @pl.when(t > 0)
        def _():
            x_load(t).wait()

        dy_load(t).wait()
        r = pl.ds(pl.multiple_of(t * TILE, TILE), TILE)
        x = a_all[0, r].astype(F32)
        a = (x * norm_scale(x)).astype(BF16)
        a_all[0, r] = a
        acc = None
        step = 512
        for c in range(ff // step):
            cols = pl.ds(c * step, step)
            gate = dot(a, w0_gu[0, :, cols])
            up = dot(a, w0_gu[1, :, cols])
            hid = (gate * sigmoid(gate) * up).astype(BF16)
            term = dot(hid, w0_d[cols])
            acc = term if acc is None else acc + term
        h = (x + acc.astype(BF16).astype(F32)).astype(BF16)
        h_all[r] = h
        wide = h.astype(F32)
        a = (wide * norm_scale(wide)).astype(BF16)
        a_all[1, r] = a
        a_t[:, r] = a.T
        d_t[:, r] = d_all[r].T
        return carry

    lax.fori_loop(0, tiles, forward, 0)

    def piece(j, which):
        if which is None:
            return pl.ds(pl.multiple_of(j * rows, rows), rows)
        return pl.ds(pl.multiple_of(j * rows + which * half, half), half)

    def copies(kind, q):
        par = lax.rem(q, 2)
        g = lax.rem(q, GSLOTS)
        if kind == 0:
            pairs = [(part.at[par, :, piece(across, d)], r1.at[par, d]) for d in range(2)]
        elif kind == 1:
            pairs = [(part.at[par, :, piece(to, None)], r2.at[par, d]) for d, to in enumerate((right, left))]
        elif kind == 2:
            own = grad.at[g, :, piece(me, None)]
            pairs = [(own, own), (own, own)]
        else:
            pairs = [(grad.at[g, :, piece(who, d)],) * 2 for d, who in enumerate((left, right))]
        return [
            pltpu.make_async_remote_copy(
                src_ref=src, dst_ref=dst, send_sem=send_sem.at[kind, d, par], recv_sem=recv_sem.at[kind, d, par],
                device_id={"dp": to}, device_id_type=pl.DeviceIdType.MESH,
            )
            for d, ((src, dst), to) in enumerate(zip(pairs, (right, left)))
        ]

    def landed(kind, q):
        par = lax.rem(q, 2)
        g = lax.rem(q, GSLOTS)
        if kind == 0:
            refs = [r1.at[par, d] for d in range(2)]
        elif kind == 1:
            refs = [r2.at[par, d] for d in range(2)]
        elif kind == 2:
            refs = [grad.at[g, :, piece(who, None)] for who in (left, right)]
        else:
            refs = [grad.at[g, :, piece(across, d)] for d in range(2)]
        for d, (ref, copy) in enumerate(zip(refs, copies(kind, q))):
            pltpu.make_async_remote_copy(
                src_ref=ref, dst_ref=ref, send_sem=send_sem.at[kind, d, par], recv_sem=recv_sem.at[kind, d, par],
                device_id={"dp": (left, right)[d]}, device_id_type=pl.DeviceIdType.MESH,
            ).wait_recv()
            copy.wait_send()

    def send(kind, q):
        for copy in copies(kind, q):
            copy.start()

    def pass_on(q):
        landed(0, q)
        par = lax.rem(q, 2)
        for d, to in enumerate((right, left)):
            at = piece(to, d)
            part[par, :, at] = (part[par, :, at].astype(F32) + r1[par, d].astype(F32)).astype(BF16)
        send(1, q)

    def finish(q):
        landed(1, q)
        par = lax.rem(q, 2)
        mine = part[par, :, piece(me, None)].astype(F32)
        grad[lax.rem(q, GSLOTS), :, piece(me, None)] = (mine + r2[par, 0].astype(F32) + r2[par, 1].astype(F32)).astype(BF16)
        send(2, q)

    def forward_on(q):
        landed(2, q)
        send(3, q)

    def out_copy(q):
        return pltpu.make_async_copy(grad.at[lax.rem(q, GSLOTS)], g_hbm.at[q], out_sem.at[lax.rem(q, 2)])

    def complete(q):
        landed(3, q)
        out_copy(q).start()

    def tile_body(layer, slot, t, with_da, fresh):
        r = pl.ds(pl.multiple_of(t * TILE, TILE), TILE)
        gu = dot(a_all[layer, r], s_gu[slot])
        gate, up = gu[:, :CHUNK], gu[:, CHUNK:]
        dhid = dot_t(d_all[r], s_d[slot]).astype(BF16).astype(F32)
        sig = sigmoid(gate)
        silu = gate * sig
        hid_all[r] = (silu * up).astype(BF16)
        dgate = (dhid * up * (sig + silu * (1.0 - sig))).astype(BF16)
        dup = (dhid * silu).astype(BF16)
        dgu_all[r, :CHUNK] = dgate
        dgu_all[r, CHUNK:] = dup
        if with_da:
            term = dot_t(jnp.concatenate([dgate, dup], axis=1), s_gu[slot])
            da[r] = jnp.where(fresh, 0.0, da[r]) + term

    def service(guard, fn, q):
        if not comm:
            return
        if guard is None:
            fn(q)
        else:
            pl.when(guard)(lambda: fn(q))

    def chunk_step(s, with_da):
        layer = top - s // chunks
        slot = lax.rem(s, 2)
        for copy in w_loads(s):
            copy.wait()

        @pl.when(s + 1 < total)
        def _():
            for copy in w_loads(s + 1):
                copy.start()

        service(s >= 3, forward_on, s - 3)
        fresh = lax.rem(s, chunks) == 0
        body = lambda t, c: (tile_body(layer, slot, t, with_da, fresh), c)[1]
        lax.fori_loop(0, tiles // 2, body, 0)
        service(s >= 2, finish, s - 2)
        lax.fori_loop(tiles // 2, tiles, body, 0)
        service(s >= 1, pass_on, s - 1)
        service(s >= 4, lambda q: out_copy(q).wait(), s - 4)
        dw = dot(a_t[...], dgu_all[...])
        part[slot, 0] = dw[:, :CHUNK].astype(BF16)
        part[slot, 1] = dw[:, CHUNK:].astype(BF16)
        dd = dot(d_t[...], hid_all[...])
        for k in range(width // CHUNK):
            b = pl.ds(k * CHUNK, CHUNK)
            part[slot, 2, b] = dd[k * CHUNK : (k + 1) * CHUNK].T.astype(BF16)
        if comm:
            send(0, s)
        else:
            pltpu.make_async_copy(part.at[slot], g_hbm.at[s], out_sem.at[slot]).start()
            pltpu.make_async_copy(part.at[slot], g_hbm.at[s], out_sem.at[slot]).wait()
        service(s >= 3, complete, s - 3)

    def turn(t, carry):
        r = pl.ds(pl.multiple_of(t * TILE, TILE), TILE)
        by_a = da[r].astype(BF16).astype(F32)
        h = h_all[r].astype(F32)
        scale = norm_scale(h)
        inner = jnp.mean(by_a * h, -1, keepdims=True)
        by_h = d_all[r].astype(F32) + (by_a * scale - h * (scale * scale * scale * inner))
        by_h = by_h.astype(BF16)
        d_all[r] = by_h
        d_t[:, r] = by_h.T
        a_t[:, r] = a_all[0, r].T
        return carry

    if comm:
        pl.semaphore_wait(barrier, 2)

    def upper(s, carry):
        chunk_step(s, True)
        return carry

    def lower(s, carry):
        chunk_step(s, False)
        return carry

    lax.fori_loop(0, chunks, upper, 0)
    lax.fori_loop(0, tiles, turn, 0)
    lax.fori_loop(chunks, total, lower, 0)

    def drain(s, carry):
        service(s <= total + 2, forward_on, s - 3)
        service(s <= total + 1, finish, s - 2)
        service(s <= total, pass_on, s - 1)
        service(None, lambda q: out_copy(q).wait(), s - 4)
        service(s <= total + 2, complete, s - 3)
        return carry

    if comm:
        lax.fori_loop(total, total + 4, drain, 0)


def gradients(n, x, dy, wg, wu, wd, comm=True):
    _, tokens, width = x.shape
    layers, _, ff = wg.shape
    assert layers == 2 and n == 4
    total = layers * ff // CHUNK
    rows = width // n
    anywhere = pl.BlockSpec(memory_space=pl.ANY)
    tiles = tokens // TILE
    return pl.pallas_call(
        functools.partial(step_kernel, n, comm),
        out_shape=jax.ShapeDtypeStruct((total, 3, width, CHUNK), BF16),
        in_specs=[anywhere] * 5,
        out_specs=anywhere,
        scratch_shapes=[
            pltpu.VMEM((2, tokens, width), BF16),
            pltpu.VMEM((width, tokens), BF16),
            pltpu.VMEM((tokens, width), BF16),
            pltpu.VMEM((width, tokens), BF16),
            pltpu.VMEM((tokens, width), F32),
            pltpu.VMEM((tokens, width), BF16),
            pltpu.VMEM((tokens, CHUNK), BF16),
            pltpu.VMEM((tokens, 2 * CHUNK), BF16),
            pltpu.VMEM((2, width, ff), BF16),
            pltpu.VMEM((ff, width), BF16),
            pltpu.VMEM((2, width, 2 * CHUNK), BF16),
            pltpu.VMEM((2, CHUNK, width), BF16),
            pltpu.VMEM((2, 3, width, CHUNK), BF16),
            pltpu.VMEM((2, 2, 3, rows // 2, CHUNK), BF16),
            pltpu.VMEM((2, 2, 3, rows, CHUNK), BF16),
            pltpu.VMEM((GSLOTS, 3, width, CHUNK), BF16),
            pltpu.SemaphoreType.DMA((4 + 2 * tiles,)),
            pltpu.SemaphoreType.DMA((2, 3)),
            pltpu.SemaphoreType.DMA((2,)),
            pltpu.SemaphoreType.DMA((4, 2, 2)),
            pltpu.SemaphoreType.DMA((4, 2, 2)),
        ],
        compiler_params=pltpu.CompilerParams(
            collective_id=0 if comm else None, has_side_effects=True, vmem_limit_bytes=67043328
        ),
        name="gradients",
    )(x, dy, wg, wu, wd)


def adamw_kernel(g_ref, *refs):
    ins, outs = refs[:9], refs[9:]
    for i in range(3):
        w, m, v = (ins[k * 3 + i][0] for k in range(3))
        if i < 2:
            g = g_ref[0, i].astype(F32)
        else:
            g = jnp.concatenate([g_ref[0, i, k * CHUNK : (k + 1) * CHUNK] for k in range(g_ref.shape[2] // CHUNK)], axis=1).astype(F32)
        m = 0.9 * m + 0.1 * g
        v = 0.95 * v + 0.05 * g * g
        step = m * lax.rsqrt(v + 1e-8) + 0.1 * w.astype(F32)
        outs[i][0] = (w.astype(F32) - 0.02 * step).astype(BF16)
        outs[3 + i][0] = m
        outs[6 + i][0] = v


def adamw(g, arrays):
    layers, width, ff = arrays[0].shape
    chunks = ff // CHUNK
    wide = pl.BlockSpec((1, width, CHUNK), lambda s: (layers - 1 - s // chunks, 0, lax.rem(s, chunks)))
    tall = pl.BlockSpec((1, CHUNK, width), lambda s: (layers - 1 - s // chunks, lax.rem(s, chunks), 0))
    specs = [wide, wide, tall] * 3
    return pl.pallas_call(
        adamw_kernel,
        grid=(layers * chunks,),
        out_shape=[jax.ShapeDtypeStruct(a.shape, a.dtype) for a in arrays],
        in_specs=[pl.BlockSpec((1, 3, width, CHUNK), lambda s: (s, 0, 0, 0))] + specs,
        out_specs=specs,
        compiler_params=pltpu.CompilerParams(vmem_limit_bytes=48 * 1024 * 1024),
        name="adamw",
    )(g, *arrays)


def solution(mesh):
    n = mesh.shape["dp"]

    def step(x, dy, *arrays):
        g = gradients(n, x, dy, *arrays[:3])
        return tuple(adamw(g, arrays))

    return jax.shard_map(
        step,
        mesh=mesh,
        in_specs=(P(("rep", "dp"), None, None),) * 2 + (P(None, None, None),) * 9,
        out_specs=(P("rep", None, None),) * 9,
        check_vma=False,
    )
```

time: 634 us -> 314 us (0.50); the launches traced: 626 us -> 314 us
  matrix products: 322 us -> 0 us
  Pallas kernels: 0 us -> 311 us
  waiting for transfers between devices: 223 us -> 0 us
  other arithmetic: 51.8 us -> 0 us
  between operations: 14.7 us -> 0.82 us
  local copies, waits for them, and re-layouts: 14.7 us -> 2.18 us
    dot_general x15 -> x0, matrix products: 322 us -> none  [the longest x5 123 us: layer(): gate = jnp.dot(a, w['w_gate'], preferred_element_type=jnp.float32)]
    pallas_call x0 -> x2, Pallas kernels: none -> 311 us  [the longest x1 263 us: gradients(): pl.pallas_call(functools.partial(step_kernel, n, comm), out_shape=jax.Sha...]
    psum x1 -> x0, waiting for transfers between devices: 223 us -> none  [step(): summed[number] = [lax.psum(by_w[name], 'dp') for name in NAMES]]
    convert_element_type x2 -> x0, other arithmetic: 44.4 us -> none  [adamw(): return ((w - 0.02 * step).astype(jnp.bfloat16), m, v)]
    unnamed x32 -> x2, local copies, waits for them, and re-layouts: 14.7 us -> 2.18 us
  transfers between devices with their start and end apart: 1 -> 0, of which waited for: 1 -> 0; matrix products, arithmetic and copies ran while one was open for 0% -> 0% of each run, Pallas kernels for 0% -> 0%
where the time goes in v1:
time: 314 us
  Pallas kernels  311 us (99%)
    pallas_call x1, Pallas kernels, gradients(): pl.pallas_call(functools.partial(step_kernel, n, comm), out_shape=jax.Sha...  263 us
    pallas_call x1, Pallas kernels, adamw(): pl.pallas_call(adamw_kernel, grid=(layers * chunks,), out_shape=[jax.Shap...  47.6 us

profile of v1, /device:TPU:112, one launch (start us, length us, event | category | flops | bytes accessed | tf_op | source)
XLA Modules:
  0.0 313.9 jit_solution(11610931771933024629)
XLA Ops:
  0.6 263.3 %gradients.1.g_ref = bf16[16,3,512,256]{3,2,1,0:T(8,128)(2,1)} custom-call(bf16[1,4096,512]{2,1,0:T(8,128)(2,1)} %x_hbm.1, bf16[1,4096,512]{2,1,0:T(8,128)(2,1)} %dy_hbm.1, bf16[2,512,2048]{2,1,0:T(8,128)(2,1)} %refs_0_.1, bf16[2,512,2048]{2,1,0:T(8,128)(2,1)} %refs_1_.1, bf16[2,2048,512]{2,1,0:T(8,128)(2,1)} %refs_2_.1), custom_call_target="tpu_custom_call" | custom-call | tf_op jit(solution)/shard_map/gradients/pallas_call | solution.py:303
  264.0 0.0 copy-start
  264.0 2.2 copy-done
  266.2 47.6 %adamw.1 = (bf16[2,512,2048]{2,1,0:T(8,128)(2,1)}, bf16[2,512,2048]{2,1,0:T(8,128)(2,1)}, bf16[2,2048,512]{2,1,0:T(8,128)(2,1)}, f32[2,512,2048]{2,1,0:T(8,128)}...) custom-call(bf16[16,3,512,256]{3,2,1,0:T(8,128)(2,1)} %gradients.1.g, ...), custom_call_target="tpu_custom_call" | custom-call | tf_op jit(solution)/shard_map/adamw/pallas_call | solution.py:360
Async XLA Ops:
  264.0 2.2 copy-start

commit v2 on v1

v2 whole, which is shorter than its diff:
```python
import functools

import jax
import jax.numpy as jnp
from jax import lax
from jax.experimental import pallas as pl
from jax.experimental.pallas import tpu as pltpu
from jax.sharding import PartitionSpec as P

F32 = jnp.float32
BF16 = jnp.bfloat16
CHUNK = 256
TILE = 1024
GSLOTS = 4
FORWARD_PIECES = 4
FORWARD_TILE = 512


def dot(a, b):
    return jnp.dot(a, b, preferred_element_type=F32)


def dot_t(a, b):
    return lax.dot_general(a, b, (((1,), (1,)), ((), ())), preferred_element_type=F32)


def sigmoid(z):
    return 0.5 * jnp.tanh(0.5 * z) + 0.5


def norm_scale(wide):
    return lax.rsqrt(jnp.mean(wide * wide, -1, keepdims=True) + 1e-6)


def step_kernel(
    n, comm,
    x_hbm, dy_hbm, wg_hbm, wu_hbm, wd_hbm, near_hbm, to_right_hbm, to_left_hbm,
    a_all, a_t, d_all, d_t, da, h_all, hid_all, dgu_all, w0_gu, w0_d, s_gu, s_d, part, r1, r2, grad,
    in_sem, w0_sem, w_sem, out_sem, send_sem, recv_sem,
):
    tokens, width = h_all.shape
    layers, _, ff = wg_hbm.shape
    chunks = ff // CHUNK
    tiles = tokens // TILE
    total = layers * chunks
    rows = width // n
    half = rows // 2
    top = layers - 1
    me = lax.axis_index("dp")
    right, left = lax.rem(me + 1, n), lax.rem(me + n - 1, n)
    across = lax.rem(me + 2, n)

    def load(src, dst, sem):
        return pltpu.make_async_copy(src, dst, sem)

    piece_ff = ff // FORWARD_PIECES

    def w0_loads(c):
        cols = pl.ds(c * piece_ff, piece_ff)
        return [
            load(wg_hbm.at[0, :, cols], w0_gu.at[0, :, cols], w0_sem.at[c, 0]),
            load(wu_hbm.at[0, :, cols], w0_gu.at[1, :, cols], w0_sem.at[c, 1]),
            load(wd_hbm.at[0, cols], w0_d.at[cols], w0_sem.at[c, 2]),
        ]

    def x_load(t):
        r = pl.ds(pl.multiple_of(t * FORWARD_TILE, FORWARD_TILE), FORWARD_TILE)
        return load(x_hbm.at[0, r], h_all.at[r], in_sem.at[t, 0])

    def dy_load(t):
        r = pl.ds(pl.multiple_of(t * FORWARD_TILE, FORWARD_TILE), FORWARD_TILE)
        return load(dy_hbm.at[0, r], d_all.at[r], in_sem.at[t, 1])

    def w_loads(s):
        layer = top - s // chunks
        c = pl.ds(pl.multiple_of(lax.rem(s, chunks) * CHUNK, CHUNK), CHUNK)
        slot = lax.rem(s, 2)
        return [
            load(wg_hbm.at[layer, :, c], s_gu.at[slot, :, pl.ds(0, CHUNK)], w_sem.at[slot, 0]),
            load(wu_hbm.at[layer, :, c], s_gu.at[slot, :, pl.ds(CHUNK, CHUNK)], w_sem.at[slot, 1]),
            load(wd_hbm.at[layer, c], s_d.at[slot], w_sem.at[slot, 2]),
        ]

    x_load(0).start()
    for c in range(FORWARD_PIECES):
        for copy in w0_loads(c):
            copy.start()
    barrier = pltpu.get_barrier_semaphore() if comm else None
    if comm:
        for other in (left, right):
            pl.semaphore_signal(barrier, inc=1, device_id={"dp": other}, device_id_type=pl.DeviceIdType.MESH)
    x_load(0).wait()

    def token_rows(t):
        return pl.ds(pl.multiple_of(t * FORWARD_TILE, FORWARD_TILE), FORWARD_TILE)

    def before(t):
        r = token_rows(t)
        x = h_all[r].astype(F32)
        a_all[0, r] = (x * norm_scale(x)).astype(BF16)

    def after(t):
        r = token_rows(t)
        h = (h_all[r].astype(F32) + da[r].astype(BF16).astype(F32)).astype(BF16)
        h_all[r] = h
        wide = h.astype(F32)
        a = (wide * norm_scale(wide)).astype(BF16)
        a_all[1, r] = a
        a_t[:, r] = a.T
        d_t[:, r] = d_all[r].T

    def forward(t, opening):
        a = a_all[0, token_rows(t)]
        acc = None
        for c in range(FORWARD_PIECES):
            cols = pl.ds(c * piece_ff, piece_ff)
            if opening:
                for copy in w0_loads(c):
                    copy.wait()
                if c == 0:
                    for other in range(tokens // FORWARD_TILE):
                        if other:
                            x_load(other).start()
                        dy_load(other).start()
                    for copy in w_loads(0):
                        copy.start()
            gate = dot(a, w0_gu[0, :, cols])
            up = dot(a, w0_gu[1, :, cols])
            if c == 0 and not opening:
                after(t - 1)
            if c == 1 and not opening:
                before(jnp.minimum(t + 1, tokens // FORWARD_TILE - 1))
            hid = (gate * sigmoid(gate) * up).astype(BF16)
            term = dot(hid, w0_d[cols])
            acc = term if acc is None else acc + term
        da[token_rows(t)] = acc

    before(0)
    forward(0, True)
    for t in range(tokens // FORWARD_TILE):
        if t:
            x_load(t).wait()
        dy_load(t).wait()
    before(1)

    def forward_rest(t, carry):
        forward(t, False)
        return carry

    lax.fori_loop(1, tokens // FORWARD_TILE, forward_rest, 0)
    after(tokens // FORWARD_TILE - 1)

    def piece(j, which):
        if which is None:
            return pl.ds(pl.multiple_of(j * rows, rows), rows)
        return pl.ds(pl.multiple_of(j * rows + which * half, half), half)

    def copies(kind, q):
        par = lax.rem(q, 2)
        g = lax.rem(q, GSLOTS)
        if kind == 0:
            pairs = [(part.at[par, :, piece(across, d)], r1.at[par, d]) for d in range(2)]
        elif kind == 1:
            pairs = [(part.at[par, :, piece(to, None)], r2.at[par, d]) for d, to in enumerate((right, left))]
        else:
            pairs = [(grad.at[g, 0], grad.at[g, 1 + d]) for d in range(2)]
        return [
            pltpu.make_async_remote_copy(
                src_ref=src, dst_ref=dst, send_sem=send_sem.at[kind, d, par], recv_sem=recv_sem.at[kind, d, par],
                device_id={"dp": to}, device_id_type=pl.DeviceIdType.MESH,
            )
            for d, ((src, dst), to) in enumerate(zip(pairs, (right, left)))
        ]

    def landed(kind, q):
        for copy in copies(kind, q):
            copy.wait_recv()
            copy.wait_send()

    def send(kind, q):
        for copy in copies(kind, q):
            copy.start()

    def pass_on(q):
        landed(0, q)
        par = lax.rem(q, 2)
        for d, to in enumerate((right, left)):
            at = piece(to, d)
            part[par, :, at] = (part[par, :, at].astype(F32) + r1[par, d].astype(F32)).astype(BF16)
        send(1, q)

    def finish(q):
        landed(1, q)
        par = lax.rem(q, 2)
        mine = part[par, :, piece(me, None)].astype(F32)
        grad[lax.rem(q, GSLOTS), 0] = (mine + r2[par, 0].astype(F32) + r2[par, 1].astype(F32)).astype(BF16)
        send(2, q)

    def out_copies(q):
        g, par = lax.rem(q, GSLOTS), lax.rem(q, 2)
        return [
            pltpu.make_async_copy(grad.at[g], near_hbm.at[q], out_sem.at[par, 0]),
            pltpu.make_async_copy(grad.at[g, 1, :, pl.ds(0, half)], to_right_hbm.at[q], out_sem.at[par, 1]),
            pltpu.make_async_copy(grad.at[g, 2, :, pl.ds(half, half)], to_left_hbm.at[q], out_sem.at[par, 2]),
        ]

    def collect(q):
        landed(2, q)
        for copy in out_copies(q):
            copy.start()

    def settle(q):
        for copy in out_copies(q):
            copy.wait()

    def tile_body(layer, slot, t, with_da, fresh):
        r = pl.ds(pl.multiple_of(t * TILE, TILE), TILE)
        gu = dot(a_all[layer, r], s_gu[slot])
        gate, up = gu[:, :CHUNK], gu[:, CHUNK:]
        dhid = dot_t(d_all[r], s_d[slot]).astype(BF16).astype(F32)
        sig = sigmoid(gate)
        silu = gate * sig
        hid_all[r] = (silu * up).astype(BF16)
        dgate = (dhid * up * (sig + silu * (1.0 - sig))).astype(BF16)
        dup = (dhid * silu).astype(BF16)
        dgu_all[r, :CHUNK] = dgate
        dgu_all[r, CHUNK:] = dup
        if with_da:
            term = dot_t(jnp.concatenate([dgate, dup], axis=1), s_gu[slot])
            da[r] = jnp.where(fresh, 0.0, da[r]) + term

    def service(guard, fn, q):
        if not comm:
            return
        if guard is None:
            fn(q)
        else:
            pl.when(guard)(lambda: fn(q))

    def chunk_step(s, with_da):
        layer = top - s // chunks
        slot = lax.rem(s, 2)
        for copy in w_loads(s):
            copy.wait()

        @pl.when(s + 1 < total)
        def _():
            for copy in w_loads(s + 1):
                copy.start()

        fresh = lax.rem(s, chunks) == 0
        body = lambda t, c: (tile_body(layer, slot, t, with_da, fresh), c)[1]
        ahead = tiles - 1
        lax.fori_loop(0, ahead, body, 0)
        service(s >= 3, finish, s - 2)
        service(s >= 4, settle, s - 4)
        service(s >= 3, collect, s - 3)
        service(s >= 1, pass_on, s - 1)
        lax.fori_loop(ahead, tiles, body, 0)
        dw = dot(a_t[...], dgu_all[...])
        part[slot, 0] = dw[:, :CHUNK].astype(BF16)
        part[slot, 1] = dw[:, CHUNK:].astype(BF16)
        dd = dot(d_t[...], hid_all[...])
        for k in range(width // CHUNK):
            b = pl.ds(k * CHUNK, CHUNK)
            part[slot, 2, b] = dd[k * CHUNK : (k + 1) * CHUNK].T.astype(BF16)
        if comm:
            send(0, s)
        service(s == 1, finish, s - 1)

    def turn(t, carry):
        r = pl.ds(pl.multiple_of(t * TILE, TILE), TILE)
        by_a = da[r].astype(BF16).astype(F32)
        h = h_all[r].astype(F32)
        scale = norm_scale(h)
        inner = jnp.mean(by_a * h, -1, keepdims=True)
        by_h = d_all[r].astype(F32) + (by_a * scale - h * (scale * scale * scale * inner))
        by_h = by_h.astype(BF16)
        d_all[r] = by_h
        d_t[:, r] = by_h.T
        a_t[:, r] = a_all[0, r].T
        return carry

    if comm:
        pl.semaphore_wait(barrier, 2)

    def upper(s, carry):
        chunk_step(s, True)
        return carry

    def lower(s, carry):
        chunk_step(s, False)
        return carry

    lax.fori_loop(0, chunks, upper, 0)
    lax.fori_loop(0, tiles, turn, 0)
    lax.fori_loop(chunks, total, lower, 0)

    if comm:
        last = total - 1
        finish(last - 1)
        settle(last - 3)
        collect(last - 2)
        pass_on(last)
        finish(last)
        settle(last - 2)
        collect(last - 1)
        collect(last)
        settle(last - 1)
        settle(last)


def gradients(n, x, dy, wg, wu, wd, comm=True):
    _, tokens, width = x.shape
    layers, _, ff = wg.shape
    assert layers == 2 and n == 4
    total = layers * ff // CHUNK
    rows = width // n
    anywhere = pl.BlockSpec(memory_space=pl.ANY)
    return pl.pallas_call(
        functools.partial(step_kernel, n, comm),
        out_shape=[
            jax.ShapeDtypeStruct((total, 3, 3, rows, CHUNK), BF16),
            jax.ShapeDtypeStruct((total, 3, rows // 2, CHUNK), BF16),
            jax.ShapeDtypeStruct((total, 3, rows // 2, CHUNK), BF16),
        ],
        in_specs=[anywhere] * 5,
        out_specs=[anywhere] * 3,
        scratch_shapes=[
            pltpu.VMEM((2, tokens, width), BF16),
            pltpu.VMEM((width, tokens), BF16),
            pltpu.VMEM((tokens, width), BF16),
            pltpu.VMEM((width, tokens), BF16),
            pltpu.VMEM((tokens, width), F32),
            pltpu.VMEM((tokens, width), BF16),
            pltpu.VMEM((tokens, CHUNK), BF16),
            pltpu.VMEM((tokens, 2 * CHUNK), BF16),
            pltpu.VMEM((2, width, ff), BF16),
            pltpu.VMEM((ff, width), BF16),
            pltpu.VMEM((2, width, 2 * CHUNK), BF16),
            pltpu.VMEM((2, CHUNK, width), BF16),
            pltpu.VMEM((2, 3, width, CHUNK), BF16),
            pltpu.VMEM((2, 2, 3, rows // 2, CHUNK), BF16),
            pltpu.VMEM((2, 2, 3, rows, CHUNK), BF16),
            pltpu.VMEM((GSLOTS, 3, 3, rows, CHUNK), BF16),
            pltpu.SemaphoreType.DMA((tokens // FORWARD_TILE, 2)),
            pltpu.SemaphoreType.DMA((FORWARD_PIECES, 3)),
            pltpu.SemaphoreType.DMA((2, 3)),
            pltpu.SemaphoreType.DMA((2, 3)),
            pltpu.SemaphoreType.DMA((3, 2, 2)),
            pltpu.SemaphoreType.DMA((3, 2, 2)),
        ],
        compiler_params=pltpu.CompilerParams(
            collective_id=0 if comm else None, has_side_effects=True, vmem_limit_bytes=67043328
        ),
        name="gradients",
    )(x, dy, wg, wu, wd)


def adamw_math(w, m, v, g):
    m = 0.9 * m + 0.1 * g
    v = 0.95 * v + 0.05 * g * g
    step = m * lax.rsqrt(v + 1e-8) + 0.1 * w
    return (w - 0.02 * step).astype(BF16), m, v


def adamw_kernel(gs, me_ref, *refs):
    parts, ins, outs = refs[:gs], refs[gs : gs + 9], refs[-9:]
    group = parts[0].shape[0]
    for j in range(group):
        cols = pl.ds(j * CHUNK, CHUNK)
        for i in range(3):
            g = parts[0][j, 0, i] if gs == 1 else jnp.concatenate([p[j, i] for p in parts], axis=0)
            at = (0, slice(None), cols) if i < 2 else (0, j)
            new = adamw_math(ins[i][at].astype(F32), ins[3 + i][at], ins[6 + i][at], g.astype(F32))
            for k in range(3):
                outs[3 * k + i][at] = new[k]


def adamw(n, me, gs, arrays, group, near, before):
    layers, width, ff = arrays[0].shape
    groups = ff // CHUNK // group
    rows = width // n
    per = CHUNK // rows

    def row(rel, me):
        ahead = jnp.where(rel == 0, 0, jnp.where(rel == 1, n - 1, 1)) if near else n // 2
        return lax.rem(me[0] + ahead, n)

    def wide_map(s, rel, c, me):
        return layers - 1 - s, row(rel, me), c

    def tall_map(s, rel, c, me):
        at = row(rel, me)
        return layers - 1 - s, c, lax.rem(at, per), at // per

    wide = pl.BlockSpec((1, rows, group * CHUNK), wide_map, pipeline_mode=pl.Buffered(2))
    tall = pl.BlockSpec((1, group, rows, CHUNK), tall_map, pipeline_mode=pl.Buffered(2))
    specs = [wide, wide, tall] * 3
    outs = [pl.BlockSpec(b.block_shape, b.index_map) for b in specs]
    if near:
        g_specs = [pl.BlockSpec((group, 1, 3, rows, CHUNK), lambda s, rel, c, me: (s * groups + c, rel, 0, 0, 0))]
    else:
        g_specs = [pl.BlockSpec((group, 3, rows // 2, CHUNK), lambda s, rel, c, me: (s * groups + c, 0, 0, 0))] * 2
    shares = 3 if near else 1
    size = layers * ff * 3 * rows * shares
    return pl.pallas_call(
        functools.partial(adamw_kernel, len(gs)),
        grid_spec=pltpu.PrefetchScalarGridSpec(
            num_scalar_prefetch=1,
            grid=(layers, shares, groups),
            in_specs=g_specs + specs + [pl.BlockSpec(memory_space=pl.ANY)] * len(before),
            out_specs=outs,
        ),
        out_shape=[jax.ShapeDtypeStruct(a.shape, a.dtype) for a in arrays],
        input_output_aliases={1 + len(gs) + 9 + i: i for i in range(len(before))},
        compiler_params=pltpu.CompilerParams(vmem_limit_bytes=67043328),
        cost_estimate=pl.CostEstimate(flops=size * 2000, bytes_accessed=size * 22, transcendentals=size),
        name="adamw_near" if near else "adamw_across",
    )(me, *gs, *arrays, *before)


def solution(mesh):
    n = mesh.shape["dp"]

    to_right = [(i, (i + 1) % n) for i in range(n)]
    to_left = [(i, (i - 1) % n) for i in range(n)]

    def step(x, dy, *arrays):
        near, for_right, for_left = gradients(n, x, dy, *arrays[:3])
        far = (lax.ppermute(for_right, "dp", to_right), lax.ppermute(for_left, "dp", to_left))
        me = lax.axis_index("dp").astype(jnp.int32).reshape(1)
        layers, ff, width = arrays[2].shape
        cut = [a.reshape(layers, ff // CHUNK, CHUNK, width) if i % 3 == 2 else a for i, a in enumerate(arrays)]
        new = adamw(n, me, (near,), cut, 8, True, ())
        new = adamw(n, me, far, cut, 4, False, new)
        return tuple(a.reshape(layers, ff, width) if i % 3 == 2 else a for i, a in enumerate(new))

    return jax.shard_map(
        step,
        mesh=mesh,
        in_specs=(P(("rep", "dp"), None, None),) * 2 + (P(None, None, None),) * 9,
        out_specs=(P("rep", None, None),) * 9,
        check_vma=False,
    )
```

time: 314 us -> 284 us (0.904)
  Pallas kernels: 311 us -> 280 us
  starting transfers between devices: 0 us -> 3.31 us
    pallas_call x2 -> x3, Pallas kernels: 311 us -> 280 us  [the longest x1 233 us: gradients(): pl.pallas_call(functools.partial(step_kernel, n, comm), out_shape=[jax.Sh...]
    ppermute x0 -> x2, starting transfers between devices: none -> 3.31 us  [the longest x1 3.21 us: step(): lax.ppermute(for_left, 'dp', to_left)]
  transfers between devices with their start and end apart: 0 -> 2, of which waited for: 0 -> 0; matrix products, arithmetic and copies ran while one was open for 0% -> 0% of each run, Pallas kernels for 0% -> 12%
where the time goes in v2:
time: 284 us
  Pallas kernels  280 us (99%)
  starting transfers between devices  3.31 us (1%)
    pallas_call x1, Pallas kernels, gradients(): pl.pallas_call(functools.partial(step_kernel, n, comm), out_shape=[jax.Sh...  233 us
    pallas_call x2, Pallas kernels, adamw(): pl.pallas_call(functools.partial(adamw_kernel, len(gs)), grid_spec=pltpu....  46.3 us
  transfers between devices with their start and end apart: 2, of which 0 were waited for; matrix products, arithmetic and copies ran while one was open for 0% of the time, Pallas kernels for 12%

profile of v2, /device:TPU:112, one launch (start us, length us, event | category | flops | bytes accessed | tf_op | source)
XLA Modules:
  0.0 283.8 jit_solution(1277271340274518167)
XLA Ops:
  0.6 233.4 %gradients.1 = (bf16[16,3,3,128,256]{4,3,2,1,0:T(8,128)(2,1)}, bf16[16,3,64,256]{3,2,1,0:T(8,128)(2,1)}, bf16[16,3,64,256]{3,2,1,0:T(8,128)(2,1)}) custom-call(bf16[1,4096,512]{2,1,0:T(8,128)(2,1)} %x_hbm.1, bf16[1,4096,512]{2,1,0:T(8,128)(2,1)} %dy_hbm.1, bf16[2,512,2048]{2,1,0:T(8,128)(2,1)} %refs_2_.3, bf16[2,512,2048]{2,1,0:T(8,128)(2,1)} %refs_3_.1, ...), custom_call_target="tpu_custom_call" | custom-call | tf_op jit(solution)/shard_map/gradients/pallas_call | solution.py:320
  234.0 0.1 collective-permute-start
  234.2 3.2 %collective-permute-start.1 = (bf16[16,3,64,256]{3,2,1,0:T(8,128)(2,1)}, bf16[16,3,64,256]{3,2,1,0:T(8,128)(2,1)}, u32[]{:S(2)}, u32[]{:S(2)}) collective-permute-start(bf16[16,3,64,256]{3,2,1,0:T(8,128)(2,1)} %get-tuple-element.31), channel_id=1, source_target_pairs={{0,3},{1,0},{2,1},{3,2},{4,7},{5,4},{6,5},{7,6},{8,11},{9,8},{10,9... | collective-permute-start | bytes 4718600 | tf_op jit(solution)/shard_map/ppermute | solution.py:431
  237.4 33.7 %adamw_near.1 = (bf16[2,512,2048]{2,1,0:T(8,128)(2,1)}, bf16[2,512,2048]{2,1,0:T(8,128)(2,1)}, bf16[2,8,256,512]{3,2,1,0:T(8,128)(2,1)}, f32[2,512,2048]{2,1,0:T...) custom-call(s32[1]{0:T(128)} %bitcast.me_ref, ...), custom_call_target="tpu_custom_call" | custom-call | flops 9437184000 | bytes 103809024 | tf_op jit(solution)/shard_map/adamw_near/pallas_call | solution.py:407
  271.1 0.0 collective-permute-done.refs_0_
  271.1 0.0 collective-permute-done.1.refs_1_
  271.1 12.6 %adamw_across.1 = (bf16[2,512,2048]{2,1,0:T(8,128)(2,1)}, bf16[2,512,2048]{2,1,0:T(8,128)(2,1)}, bf16[2,8,256,512]{3,2,1,0:T(8,128)(2,1)}, f32[2,512,2048]{2,1,0...) custom-call(s32[1]{0:T(128)} %bitcast.me_ref, ...), custom_call_target="tpu_custom_call", output_to_operand_aliasing={{0}: (12, {}), {1}: (13, {}), {2}: (14, {}), {3}: (15, {}),... | custom-call | flops 3145728000 | bytes 34603008 | tf_op jit(solution)/shard_map/adamw_across/pallas_call | solution.py:407
Async XLA Ops:
  234.0 37.0 %collective-permute-start = (bf16[16,3,64,256]{3,2,1,0:T(8,128)(2,1)}, bf16[16,3,64,256]{3,2,1,0:T(8,128)(2,1)}, u32[]{:S(2)}, u32[]{:S(2)}) collective-permute-start(bf16[16,3,64,256]{3,2,1,0:T(8,128)(2,1)} %get-tuple-element.30), channel_id=1, source_target_pairs={{0,1},{1,2},{2,3},{3,0},{4,5},{5,6},{6,7},{7,4},{8,9},{9,10},{10,1... | collective-permute-start | bytes 4718600 | tf_op jit(solution)/shard_map/ppermute | solution.py:431
  234.2 36.9 %collective-permute-start.1 = (bf16[16,3,64,256]{3,2,1,0:T(8,128)(2,1)}, bf16[16,3,64,256]{3,2,1,0:T(8,128)(2,1)}, u32[]{:S(2)}, u32[]{:S(2)}) collective-permute-start(bf16[16,3,64,256]{3,2,1,0:T(8,128)(2,1)} %get-tuple-element.31), channel_id=1, source_target_pairs={{0,3},{1,0},{2,1},{3,2},{4,7},{5,4},{6,5},{7,6},{8,11},{9,8},{10,9... | collective-permute-start | bytes 4718600 | tf_op jit(solution)/shard_map/ppermute | solution.py:431

commit v3 on v2

--- a/solution.py
+++ b/solution.py
@@ -433,7 +433,7 @@
         layers, ff, width = arrays[2].shape
         cut = [a.reshape(layers, ff // CHUNK, CHUNK, width) if i % 3 == 2 else a for i, a in enumerate(arrays)]
         new = adamw(n, me, (near,), cut, 8, True, ())
-        new = adamw(n, me, far, cut, 4, False, new)
+        new = adamw(n, me, far, cut, 8, False, new)
         return tuple(a.reshape(layers, ff, width) if i % 3 == 2 else a for i, a in enumerate(new))
 
     return jax.shard_map(

time: 284 us -> 283 us (level)
  no operation moved by 1% of the time
where the time goes in v3:
time: 283 us
  Pallas kernels  279 us (99%)
  starting transfers between devices  3.31 us (1%)
    pallas_call x1, Pallas kernels, gradients(): pl.pallas_call(functools.partial(step_kernel, n, comm), out_shape=[jax.Sh...  233 us
    pallas_call x2, Pallas kernels, adamw(): pl.pallas_call(functools.partial(adamw_kernel, len(gs)), grid_spec=pltpu....  45.8 us
  transfers between devices with their start and end apart: 2, of which 0 were waited for; matrix products, arithmetic and copies ran while one was open for 0% of the time, Pallas kernels for 12%

profile of v3, /device:TPU:112, one launch (start us, length us, event | category | flops | bytes accessed | tf_op | source)
XLA Modules:
  0.0 283.3 jit_solution(2969002330813584649)
XLA Ops:
  0.6 233.4 %gradients.1 = (bf16[16,3,3,128,256]{4,3,2,1,0:T(8,128)(2,1)}, bf16[16,3,64,256]{3,2,1,0:T(8,128)(2,1)}, bf16[16,3,64,256]{3,2,1,0:T(8,128)(2,1)}) custom-call(bf16[1,4096,512]{2,1,0:T(8,128)(2,1)} %x_hbm.1, bf16[1,4096,512]{2,1,0:T(8,128)(2,1)} %dy_hbm.1, bf16[2,512,2048]{2,1,0:T(8,128)(2,1)} %refs_2_.3, bf16[2,512,2048]{2,1,0:T(8,128)(2,1)} %refs_3_.1, ...), custom_call_target="tpu_custom_call" | custom-call | tf_op jit(solution)/shard_map/gradients/pallas_call | solution.py:320
  234.0 0.1 collective-permute-start
  234.2 3.2 %collective-permute-start.1 = (bf16[16,3,64,256]{3,2,1,0:T(8,128)(2,1)}, bf16[16,3,64,256]{3,2,1,0:T(8,128)(2,1)}, u32[]{:S(2)}, u32[]{:S(2)}) collective-permute-start(bf16[16,3,64,256]{3,2,1,0:T(8,128)(2,1)} %get-tuple-element.31), channel_id=1, source_target_pairs={{0,3},{1,0},{2,1},{3,2},{4,7},{5,4},{6,5},{7,6},{8,11},{9,8},{10,9... | collective-permute-start | bytes 4718600 | tf_op jit(solution)/shard_map/ppermute | solution.py:431
  237.4 33.7 %adamw_near.1 = (bf16[2,512,2048]{2,1,0:T(8,128)(2,1)}, bf16[2,512,2048]{2,1,0:T(8,128)(2,1)}, bf16[2,8,256,512]{3,2,1,0:T(8,128)(2,1)}, f32[2,512,2048]{2,1,0:T...) custom-call(s32[1]{0:T(128)} %bitcast.me_ref, ...), custom_call_target="tpu_custom_call" | custom-call | flops 9437184000 | bytes 103809024 | tf_op jit(solution)/shard_map/adamw_near/pallas_call | solution.py:407
  271.1 0.0 collective-permute-done.refs_0_
  271.1 0.0 collective-permute-done.1.refs_1_
  271.1 12.1 %adamw_across.1 = (bf16[2,512,2048]{2,1,0:T(8,128)(2,1)}, bf16[2,512,2048]{2,1,0:T(8,128)(2,1)}, bf16[2,8,256,512]{3,2,1,0:T(8,128)(2,1)}, f32[2,512,2048]{2,1,0...) custom-call(s32[1]{0:T(128)} %bitcast.me_ref, ...), custom_call_target="tpu_custom_call", output_to_operand_aliasing={{0}: (12, {}), {1}: (13, {}), {2}: (14, {}), {3}: (15, {}),... | custom-call | flops 3145728000 | bytes 34603008 | tf_op jit(solution)/shard_map/adamw_across/pallas_call | solution.py:407
Async XLA Ops:
  234.0 37.0 %collective-permute-start = (bf16[16,3,64,256]{3,2,1,0:T(8,128)(2,1)}, bf16[16,3,64,256]{3,2,1,0:T(8,128)(2,1)}, u32[]{:S(2)}, u32[]{:S(2)}) collective-permute-start(bf16[16,3,64,256]{3,2,1,0:T(8,128)(2,1)} %get-tuple-element.30), channel_id=1, source_target_pairs={{0,1},{1,2},{2,3},{3,0},{4,5},{5,6},{6,7},{7,4},{8,9},{9,10},{10,1... | collective-permute-start | bytes 4718600 | tf_op jit(solution)/shard_map/ppermute | solution.py:431
  234.2 36.9 %collective-permute-start.1 = (bf16[16,3,64,256]{3,2,1,0:T(8,128)(2,1)}, bf16[16,3,64,256]{3,2,1,0:T(8,128)(2,1)}, u32[]{:S(2)}, u32[]{:S(2)}) collective-permute-start(bf16[16,3,64,256]{3,2,1,0:T(8,128)(2,1)} %get-tuple-element.31), channel_id=1, source_target_pairs={{0,3},{1,0},{2,1},{3,2},{4,7},{5,4},{6,5},{7,6},{8,11},{9,8},{10,9... | collective-permute-start | bytes 4718600 | tf_op jit(solution)/shard_map/ppermute | solution.py:431
